TPU v7x, 32 devices: a whole 2x2x4 slice. The times are simulated.
32 devices in a mesh: dp: 16 (over z, y, x), sub: 2 (over core).
Axes of the slice: x: 2, y: 2, z: 4, core: 2. Of those that a mesh axis runs over, the one named last changes fastest.
Arguments:
- projections: float32 [6144, 128], P(('dp', 'sub')), may hold values from -6 to 6
- partner: int32 [6144], P(('dp', 'sub')), may hold values from 0 to 6143, as said below
Outputs:
- loss: float32 [], replicated
- grad_projections: float32 [6144, 128], P(('dp', 'sub'))
Inputs may be any that keep to these rules, and one draw needn't show every extreme that they name: partner pairs the views: partner[partner[i]] = i and partner[i] != i for every view.
All inputs are finite; a program needn't handle non-finite values.
Results may differ from a plain program's by a relative error of at most 0.0003.
The roundings to bfloat16 on the way count: a program that leaves them out, or rounds other values in their place, can miss the bound.
Values may be sent and summed in bfloat16 or wider, within the bound.
A program may use at most 128 MiB of HBM per device.

v0:
```python
import functools
import math

import jax
import jax.numpy as jnp
from jax import lax
from jax.experimental import pallas as pl
from jax.experimental.pallas import tpu as pltpu
from jax.sharding import PartitionSpec as P

TAU = 0.1
SHIFT = 10.0
EPS = 1e-06
LANES = 128
MESH = pl.DeviceIdType.MESH
LINE = 4

FORWARD = (
    (0, 0, 0), (1, 0, 0), (2, 0, 0), (3, 0, 0), (0, 0, 1), (0, 1, 0), (0, 1, 1), (1, 0, 1),
    (1, 1, 0), (1, 1, 1), (2, 0, 1), (2, 1, 0), (2, 1, 1), (3, 0, 1), (3, 1, 0), (3, 1, 1),
)
EARLY = 4
WAYS = 7


def plan():
    at = {step: i for i, step in enumerate(FORWARD)}
    chunks = []
    for place in range(LINE):
        for dx in range(2):
            for dy in range(2):
                chunks.append((max(at[(place, dy, dx)], at[(place, dx, dy)]), (place, dx, dy)))
    chunks.sort()
    out = []
    for i, step in enumerate(FORWARD):
        out.append(("step", step))
        if i >= EARLY and chunks and chunks[0][0] < i:
            out.append(("chunk", chunks.pop(0)[1]))
    out.extend(("chunk", c) for _, c in chunks)
    return out


def kernel(
    groups, p_hbm, partner_hbm, loss_ref, grad_ref, p_ref, partner_ref,
    blocks, scores, totals, accum, pos, gsum, unit_s, mates, fetched, send, recv, rsend, rrecv,
):
    rows = p_hbm.shape[0]
    pair = 2 * rows
    tiles = pair // LANES
    spare = 2 * LANES - rows
    d = lax.axis_index("dp")
    c = lax.axis_index("sub")
    z = d // 4
    y = (d // 2) % 2
    x = d % 2
    me = d * 2 + c
    first = x * (1 - c) + y * c
    last = y * (1 - c) + x * c
    half = z // 2

    def place_z(k):
        return (z, z + 1 - 2 * (z % 2), 2 - half, 3 - 3 * half)[k]

    def chip_of(zz, f, l):
        return zz * 4 + f * (1 + c) + l * (2 - c)

    flip = lambda v, n: v + n * (1 - 2 * v)
    near_first = (chip_of(z, flip(first, 1), last), c)
    near_last = (chip_of(z, first, flip(last, 1)), c)
    diagonal = (chip_of(z, flip(first, 1), flip(last, 1)), c)
    sibling = (d, 1 - c)
    line = [(chip_of(place_z(k), first, last), c) for k in (1, 2, 3)]

    fetch = pltpu.make_async_copy(p_hbm, p_ref, fetched.at[0])
    fetch.start()
    fetch_mates = pltpu.make_async_copy(partner_hbm, partner_ref, fetched.at[1])
    fetch_mates.start()
    barrier = pltpu.get_barrier_semaphore()
    peers = (*line, near_first, near_last, diagonal, sibling)
    for dev in peers:
        pl.semaphore_signal(barrier, inc=1, device_id=dev, device_id_type=MESH)

    accum[...] = jnp.zeros_like(accum)
    pos[...] = jnp.zeros_like(pos)
    gsum[...] = jnp.zeros_like(gsum)
    mine = pl.ds(pl.multiple_of(c * spare, 8), rows)
    fetch.wait()
    p = p_ref[...]
    inverse = lax.rsqrt(jnp.sum(p * p, axis=1, keepdims=True) + EPS)
    unit = p * inverse
    blocks[me] = unit.astype(jnp.bfloat16)
    unit_s[...] = unit
    fetch_mates.wait()
    spread = jnp.broadcast_to(partner_ref[...].astype(jnp.float32), (LANES, rows)).T
    mates[...] = spread.astype(jnp.int32) - lax.broadcasted_iota(jnp.int32, (rows, LANES), 1)

    pl.semaphore_wait(barrier, len(peers))

    def copy(b, dev, i, way):
        return pltpu.make_async_remote_copy(
            src_ref=blocks.at[b],
            dst_ref=blocks.at[b],
            send_sem=send.at[i, way],
            recv_sem=recv.at[b],
            device_id=dev,
            device_id_type=MESH,
        )

    def sends(step, act):
        k, dl, df = step
        i = FORWARD.index(step)
        zz = place_z(k)
        b = chip_of(zz, flip(first, df), flip(last, dl)) * 2 + c
        if (dl, df) == (0, 0):
            if k == 0:
                for way, dev in enumerate(line):
                    act(copy(b, dev, i, way))
            act(copy(b, diagonal, i, 5))
            act(copy(b, near_first, i, 3))
            act(copy(b, near_last, i, 4))
        act(copy(b, sibling, i, 6))
        return b

    def forward(step):
        k, dl, df = step
        if (k, dl, df) != (0, 0, 0):
            b = chip_of(place_z(k), flip(first, df), flip(last, dl)) * 2 + c
            copy(b, sibling, 0, 0).wait_recv()
        sends(step, lambda one: one.start())

    def chip_at(chunk):
        k, dx, dy = chunk
        return place_z(k) * 4 + flip(y, dy) * 2 + flip(x, dx)

    def pair_of(chip):
        return blocks[pl.ds(2 * chip, 2)].reshape(pair, LANES)

    scale = math.log2(math.e) / TAU

    def chunk_forward(n, chunk):
        chip = chip_at(chunk)
        copy(chip * 2 + 1 - c, sibling, 0, 0).wait_recv()
        dots = lax.dot_general(
            blocks[me], pair_of(chip), (((1,), (1,)), ((), ())), preferred_element_type=jnp.float32
        )
        powers = jnp.exp2(dots * scale - SHIFT * math.log2(math.e))
        if chunk == (0, 0, 0):
            cols = lax.broadcasted_iota(jnp.int32, (rows, pair), 1)
            at = lax.broadcasted_iota(jnp.int32, (rows, pair), 0) + c * rows
            powers = jnp.where(cols == at, 0.0, powers)
        scores[n] = powers
        total = accum[mine, :]
        found = pos[...]
        for t in range(tiles):
            part = slice(t * LANES, (t + 1) * LANES)
            total = total + powers[:, part]
            hit = mates[...] == chip * pair + t * LANES
            found = found + jnp.where(hit, dots[:, part], 0.0)
        accum[mine, :] = total
        pos[...] = found

    order = []
    for what, item in plan():
        if what == "step":
            forward(item)
        else:
            chunk_forward(len(order), item)
            order.append(item)

    every = accum[...]
    totals[me, :, 0 : 2 * LANES] = jnp.sum(every.T, axis=0, keepdims=True)
    totals[me, :, 2 * LANES : 3 * LANES] = jnp.sum(pos[...], axis=0, keepdims=True) / TAU

    def share(j):
        to = lax.rem(me + j, groups)
        return pltpu.make_async_remote_copy(
            src_ref=totals.at[me],
            dst_ref=totals.at[me],
            send_sem=rsend.at[j],
            recv_sem=rrecv.at[me],
            device_id=(to // 2, to % 2),
            device_id_type=MESH,
        )

    def shared(b):
        return pltpu.make_async_remote_copy(
            src_ref=totals.at[b],
            dst_ref=totals.at[b],
            send_sem=rsend.at[0],
            recv_sem=rrecv.at[b],
            device_id=sibling,
            device_id_type=MESH,
        )

    @pl.loop(1, groups)
    def _(j):
        share(j).start()

    row_scale = (1.0 / TAU) / jnp.sum(accum[mine, :], axis=1, keepdims=True)
    low = lax.broadcasted_iota(jnp.int32, (1, LANES), 1) < rows - LANES

    def columns(chip):
        a, b = totals[2 * chip], totals[2 * chip + 1]
        return (
            a[:, :LANES],
            jnp.where(low, a[:, LANES : 2 * LANES], b[:, :LANES]),
            b[:, LANES : 2 * LANES],
        )

    for n, chunk in enumerate(order):
        chip = chip_at(chunk)
        shared(2 * chip + 1 - c).wait_recv()
        if chunk != (0, 0, 0):
            shared(2 * chip + c).wait_recv()
        powers = scores[n]
        parts = []
        for t, column in enumerate(columns(chip)):
            weight = powers[:, t * LANES : (t + 1) * LANES] * (row_scale + (1.0 / TAU) / column)
            hit = mates[...] == chip * pair + t * LANES
            parts.append(jnp.where(hit, weight - 2.0 / TAU, weight).astype(jnp.bfloat16))
        gsum[...] += jnp.dot(
            jnp.concatenate(parts, axis=1), pair_of(chip), preferred_element_type=jnp.float32
        )

    grown = gsum[...]
    unit = unit_s[...]
    p = p_ref[...]
    inverse = lax.rsqrt(jnp.sum(p * p, axis=1, keepdims=True) + EPS)
    inner = jnp.sum(unit * grown, axis=1, keepdims=True)
    grad_ref[...] = inverse * (grown - unit * inner)

    logs = jnp.zeros((1, LANES), jnp.float32)
    for chip in range(groups // 2):
        for column in columns(chip):
            logs = logs + jnp.log(column)
        for core in range(2):
            logs = logs - totals[2 * chip + core][:, 2 * LANES : 3 * LANES]
    loss_ref[0, 0] = jnp.sum(logs) / (rows * groups) + SHIFT

    for step in FORWARD:
        sends(step, lambda one: one.wait_send())

    @pl.loop(1, groups)
    def _(j):
        share(j).wait_send()


def fused(projections, partner):
    rows, width = projections.shape
    groups = lax.axis_size(("dp", "sub"))
    chips = groups // 2
    loss, grad = pl.pallas_call(
        functools.partial(kernel, groups),
        out_shape=(
            jax.ShapeDtypeStruct((1, 1), jnp.float32),
            jax.ShapeDtypeStruct((rows, width), jnp.float32),
        ),
        in_specs=[pl.BlockSpec(memory_space=pl.ANY)] * 2,
        out_specs=(
            pl.BlockSpec(memory_space=pltpu.SMEM),
            pl.BlockSpec(memory_space=pltpu.VMEM),
        ),
        scratch_shapes=[
            pltpu.VMEM((rows, width), jnp.float32),
            pltpu.VMEM((1, rows), jnp.int32),
            pltpu.VMEM((groups, rows, width), jnp.bfloat16),
            pltpu.VMEM((chips, rows, 2 * rows), jnp.float32),
            pltpu.VMEM((groups, 1, 3 * LANES), jnp.float32),
            pltpu.VMEM((2 * LANES, LANES), jnp.float32),
            pltpu.VMEM((rows, LANES), jnp.float32),
            pltpu.VMEM((rows, width), jnp.float32),
            pltpu.VMEM((rows, width), jnp.float32),
            pltpu.VMEM((rows, LANES), jnp.int32),
            pltpu.SemaphoreType.DMA((2,)),
            pltpu.SemaphoreType.DMA((len(FORWARD), WAYS)),
            pltpu.SemaphoreType.DMA((groups,)),
            pltpu.SemaphoreType.DMA((groups,)),
            pltpu.SemaphoreType.DMA((groups,)),
        ],
        compiler_params=pltpu.CompilerParams(collective_id=0, has_side_effects=True),
    )(projections, partner.reshape(1, rows))
    return loss.reshape(()), grad


def general(projections, partner):
    rows = projections.shape[0]
    axes = ("dp", "sub")
    inverse = lax.rsqrt(jnp.sum(projections * projections, axis=1) + EPS)
    unit = projections * inverse[:, None]
    low = unit.astype(jnp.bfloat16)
    everyone = lax.all_gather(low, axes, axis=0, tiled=True)
    columns = jnp.arange(everyone.shape[0], dtype=jnp.int32)
    ids = lax.axis_index(axes) * rows + jnp.arange(rows, dtype=jnp.int32)
    score = (
        lax.dot_general(
            low, everyone, (((1,), (1,)), ((), ())), preferred_element_type=jnp.float32
        )
        / TAU
    )
    diag = columns[None, :] == ids[:, None]
    hit = columns[None, :] == partner[:, None]
    total = jnp.sum(jnp.where(diag, 0.0, jnp.exp(score - SHIFT)), axis=1)
    found = jnp.sum(jnp.where(hit, score, 0.0), axis=1)
    lse = jnp.log(total) + SHIFT
    lse_all = lax.all_gather(lse, axes, axis=0, tiled=True)
    loss = lax.psum(jnp.sum(lse - found), axes) / everyone.shape[0]
    weight = jnp.exp(score - lse[:, None]) + jnp.exp(score - lse_all[None, :])
    weight = weight - 2.0 * hit.astype(jnp.float32)
    weight = jnp.where(diag, 0.0, weight / TAU).astype(jnp.bfloat16)
    grown = jnp.dot(weight, everyone, preferred_element_type=jnp.float32)
    inner = jnp.sum(unit * grown, axis=1)
    return loss, inverse[:, None] * (grown - unit * inner[:, None])


def solution(mesh):
    small = mesh.shape["dp"] == 4 * LINE and mesh.shape["sub"] == 2

    def body(projections, partner):
        rows, width = projections.shape
        fits = width == LANES and LANES < rows < 2 * LANES and (2 * rows) % LANES == 0
        return (fused if small and fits else general)(projections, partner)

    return jax.shard_map(
        body,
        mesh=mesh,
        in_specs=(P(("dp", "sub"), None), P(("dp", "sub"))),
        out_specs=(P(), P(("dp", "sub"), None)),
        check_vma=False,
    )
```

profile of v0, /device:TPU:0, one launch (start us, length us, event | category | flops | bytes accessed | tf_op | source)
XLA Modules:
  0.0 30.7 jit_solution(2473101369552525407)
XLA Ops:
  0.6 26.7 %shard_map.41 = (f32[1,1]{1,0:T(1,128)}, f32[192,128]{1,0:T(8,128)}) custom-call(f32[192,128]{1,0:T(8,128)} %p_hbm.1, s32[1,192]{1,0:T(1,128)} %bitcast.2), custom_call_target="tpu_custom_call" | custom-call | tf_op jit(solution)/shard_map/pallas_call | solution.py:252
  28.1 1.5 %copy.7 = f32[192,128]{1,0:T(8,128)} copy(f32[192,128]{1,0:T(8,128)} %get-tuple-element.9) | data formatting | bytes 196608
where the time goes:
time: 30.9 us; the launch traced here: 30.7 us
  Pallas kernels  26.7 us (86%)
  between operations  2.45 us (8%)
  local copies, waits for them, and re-layouts  1.54 us (5%)
    pallas_call x1, Pallas kernels, fused(): pl.pallas_call(functools.partial(kernel, groups), out_shape=(jax.ShapeDty...  26.7 us
    unnamed x1, local copies, waits for them, and re-layouts  1.54 us

commit v1 on v0

v1 whole, which is shorter than its diff:
```python
import functools
import math

import jax
import jax.numpy as jnp
from jax import lax
from jax.experimental import pallas as pl
from jax.experimental.pallas import tpu as pltpu
from jax.sharding import PartitionSpec as P

TAU = 0.1
SHIFT = 10.0
EPS = 1e-06
LANES = 128
MESH = pl.DeviceIdType.MESH
LINE = 4

ORDER = (
    (0, 0, 0), (0, 1, 0), (0, 0, 1), (1, 0, 0), (2, 0, 0), (0, 1, 1), (1, 1, 0), (1, 0, 1),
    (2, 1, 0), (2, 0, 1), (3, 0, 0), (1, 1, 1), (2, 1, 1), (3, 1, 0), (3, 0, 1), (3, 1, 1),
)


def kernel(
    groups, p_hbm, partner_hbm, loss_ref, grad_ref, p_ref, partners,
    blocks, scores, totals, frame, gsum, unit_s, mates, mates_t,
    fetched, send, recv, tsend, trecv, psend, precv, near_in, two_in, three_in,
):
    rows = p_hbm.shape[0]
    pair = 2 * rows
    tiles = pair // LANES
    spare = 2 * LANES - rows
    chips = groups // 2
    d = lax.axis_index("dp")
    c = lax.axis_index("sub")
    z = d // 4
    y = (d // 2) % 2
    x = d % 2
    me = d * 2 + c
    flip = lambda v, n: v + n * (1 - 2 * v)
    inner = ((z + 1) // 2) % 2
    across = 3 - z
    skip = (z + 2) % 4
    places = (
        z,
        z + 1 - 2 * (z % 2),
        inner * across + (1 - inner) * skip,
        inner * skip + (1 - inner) * across,
    )

    def chip_at(chip):
        k, dx, dy = chip
        return places[k] * 4 + flip(y, dy) * 2 + flip(x, dx)

    near_x = (chip_at((0, 1, 0)), c)
    near_y = (chip_at((0, 0, 1)), c)
    diagonal = (chip_at((0, 1, 1)), c)
    mate = (chip_at((1, 0, 0)), c)
    at_across = (across * 4 + y * 2 + x, c)
    at_skip = (skip * 4 + y * 2 + x, c)
    sibling = (d, 1 - c)

    fetch = pltpu.make_async_copy(p_hbm, p_ref, fetched.at[0])
    fetch.start()
    fetch_mates = pltpu.make_async_copy(partner_hbm, partners.at[c], fetched.at[1])
    fetch_mates.start()
    barrier = pltpu.get_barrier_semaphore()
    signal = lambda sem, dev: pl.semaphore_signal(sem, inc=1, device_id=dev, device_id_type=MESH)
    for dev in (near_x, near_y, mate, sibling):
        signal(barrier, dev)

    @pl.when(inner == 1)
    def _():
        signal(barrier, at_across)

    gsum[...] = jnp.zeros_like(gsum)
    fetch.wait()
    p = p_ref[...]
    inverse = lax.rsqrt(jnp.sum(p * p, axis=1, keepdims=True) + EPS)
    unit = p * inverse
    blocks[me] = unit.astype(jnp.bfloat16)
    unit_s[...] = unit
    fetch_mates.wait()
    spread = jnp.broadcast_to(partners[c].astype(jnp.float32), (LANES, rows)).T
    mates[...] = spread.astype(jnp.int32) - lax.broadcasted_iota(jnp.int32, (rows, LANES), 1)

    def copy(b, dev):
        return pltpu.make_async_remote_copy(
            src_ref=blocks.at[b],
            dst_ref=blocks.at[b],
            send_sem=send,
            recv_sem=recv.at[b],
            device_id=dev,
            device_id_type=MESH,
        )

    pl.semaphore_wait(barrier, 4 + inner)
    copy(me, near_x).start()
    copy(me, near_y).start()
    copy(me, mate).start()

    @pl.when(inner == 1)
    def _():
        copy(me, at_across).start()
        signal(two_in, mate)
        signal(two_in, at_across)

    signal(near_in, near_x)
    copy(me, sibling).start()
    swap = pltpu.make_async_remote_copy(
        src_ref=partners.at[c],
        dst_ref=partners.at[c],
        send_sem=psend,
        recv_sem=precv,
        device_id=sibling,
        device_id_type=MESH,
    )
    swap.start()
    pl.semaphore_wait(two_in, 1)

    @pl.when(inner == 1)
    def _():
        signal(three_in, mate)

    copy(me, at_skip).start()
    pl.semaphore_wait(near_in, 1)
    copy(me, diagonal).start()

    @pl.when(inner == 0)
    def _():
        pl.semaphore_wait(three_in, 1)
        copy(me, at_across).start()

    def pair_of(chip):
        return blocks[pl.ds(2 * chip, 2)].reshape(pair, LANES)

    scale = math.log2(math.e) / TAU
    power = lambda dots: jnp.exp2(dots * scale - SHIFT * math.log2(math.e))
    nt = (((1,), (1,)), ((), ()))

    swap.wait_recv()
    copy(d * 2 + 1 - c, sibling).wait_recv()
    both = jnp.concatenate([partners[0], partners[1]], axis=1)
    mates_t[...] = both - lax.broadcasted_iota(jnp.int32, (rows, pair), 0)
    sums = [jnp.zeros((8, pair), jnp.float32), jnp.zeros((8, pair), jnp.float32)]
    fold = lambda v: jnp.sum(v.reshape(rows // 8, 8, pair), axis=0)

    def add(chip):
        b = chip_at(chip) * 2 + c
        dots = lax.dot_general(
            blocks[b], pair_of(d), nt, preferred_element_type=jnp.float32
        )
        powers = power(dots)
        if chip == (0, 0, 0):
            cols = lax.broadcasted_iota(jnp.int32, (rows, pair), 1)
            at = lax.broadcasted_iota(jnp.int32, (rows, pair), 0) + c * rows
            powers = jnp.where(cols == at, 0.0, powers)
        sums[0] = sums[0] + fold(powers)
        sums[1] = sums[1] + fold(jnp.where(mates_t[...] == b * rows, dots, 0.0))

    def keep(chip):
        at_chip = chip_at(chip)
        if chip != (0, 0, 0):
            copy(at_chip * 2 + 1 - c, sibling).wait_recv()
        dots = lax.dot_general(
            blocks[me], pair_of(at_chip), nt, preferred_element_type=jnp.float32
        )
        powers = power(dots)
        if chip == (0, 0, 0):
            cols = lax.broadcasted_iota(jnp.int32, (rows, pair), 1)
            at = lax.broadcasted_iota(jnp.int32, (rows, pair), 0) + c * rows
            powers = jnp.where(cols == at, 0.0, powers)
        scores[ORDER.index(chip)] = powers

    def arrive(chip, *devs):
        b = chip_at(chip) * 2 + c
        copy(b, sibling).wait_recv()
        for dev in devs:
            copy(b, dev).start()
        copy(b, sibling).start()

    add((0, 0, 0))
    arrive((0, 1, 0), mate)
    arrive((0, 0, 1), mate)
    arrive((1, 0, 0))
    keep((0, 0, 0))
    arrive((2, 0, 0), diagonal, near_x, near_y)
    add((0, 1, 0))
    arrive((0, 1, 1), mate)
    add((0, 0, 1))
    add((1, 0, 0))
    add((2, 0, 0))
    arrive((3, 0, 0), diagonal, near_x, near_y)
    add((0, 1, 1))
    add((3, 0, 0))
    keep((0, 1, 0))
    keep((0, 0, 1))
    late = [(1, 1, 0), (1, 0, 1), (2, 1, 0), (2, 0, 1), (1, 1, 1), (2, 1, 1), (3, 1, 0), (3, 0, 1), (3, 1, 1)]
    fill = [(1, 0, 0), (2, 0, 0), (0, 1, 1), (3, 0, 0)]
    for n, chip in enumerate(late):
        arrive(chip)
        add(chip)
        if n < len(fill):
            keep(fill[n])

    found = jnp.sum(sums[1], axis=0, keepdims=True)
    totals[me, :, 0:pair] = jnp.sum(sums[0], axis=0, keepdims=True)
    totals[me, :, pair : pair + LANES] = (
        sum(found[:, t * LANES : (t + 1) * LANES] for t in range(tiles)) / TAU
    )

    def share(dev):
        return pltpu.make_async_remote_copy(
            src_ref=totals.at[me],
            dst_ref=totals.at[me],
            send_sem=tsend,
            recv_sem=trecv.at[d],
            device_id=dev,
            device_id_type=MESH,
        )

    for chip in ORDER[::-1]:
        if chip != (0, 0, 0):
            share((chip_at(chip), c)).start()
        share((chip_at(chip), 1 - c)).start()

    def shared(chip):
        at = totals.at[d * 2 + 1 - c] if chip == (0, 0, 0) else totals.at[pl.ds(2 * chip_at(chip), 2)]
        return pltpu.make_async_remote_copy(
            src_ref=at,
            dst_ref=at,
            send_sem=tsend,
            recv_sem=trecv.at[chip_at(chip)],
            device_id=sibling,
            device_id_type=MESH,
        )

    for chip in late:
        keep(chip)

    logs = jnp.zeros((1, pair), jnp.float32)
    matched = jnp.zeros((1, LANES), jnp.float32)
    for chip in ORDER:
        at_chip = chip_at(chip)
        shared(chip).wait_recv()
        a, b = totals[2 * at_chip], totals[2 * at_chip + 1]
        column = a[:, :pair] + b[:, :pair]
        logs = logs + jnp.log(column)
        matched = matched + a[:, pair:] + b[:, pair:]
        if chip == (0, 0, 0):
            own = jnp.where(c == 0, column[:, : 2 * LANES], column[:, pair - 2 * LANES :])
            frame[...] = jnp.broadcast_to((1.0 / TAU) / own, (LANES, 2 * LANES)).T
            row_scale = frame[pl.ds(pl.multiple_of(c * spare, 8), rows), :]
        powers = scores[ORDER.index(chip)]
        col_scale = (1.0 / TAU) / column
        parts = []
        for t in range(tiles):
            part = slice(t * LANES, (t + 1) * LANES)
            weight = powers[:, part] * (row_scale + col_scale[:, part])
            hit = mates[...] == at_chip * pair + t * LANES
            parts.append(jnp.where(hit, weight - 2.0 / TAU, weight).astype(jnp.bfloat16))
        gsum[...] += jnp.dot(
            jnp.concatenate(parts, axis=1), pair_of(at_chip), preferred_element_type=jnp.float32
        )

    grown = gsum[...]
    unit = unit_s[...]
    p = p_ref[...]
    inverse = lax.rsqrt(jnp.sum(p * p, axis=1, keepdims=True) + EPS)
    inner_product = jnp.sum(unit * grown, axis=1, keepdims=True)
    grad_ref[...] = inverse * (grown - unit * inner_product)
    loss_ref[0, 0] = (jnp.sum(logs) - jnp.sum(matched)) / (rows * groups) + SHIFT

    swap.wait_send()
    sent = blocks.at[pl.ds(0, groups - 1)]
    pltpu.make_async_remote_copy(
        src_ref=sent, dst_ref=sent, send_sem=send, recv_sem=recv.at[0], device_id=sibling,
        device_id_type=MESH,
    ).wait_send()
    told = totals.at[pl.ds(0, groups - 1)]
    pltpu.make_async_remote_copy(
        src_ref=told, dst_ref=told, send_sem=tsend, recv_sem=trecv.at[0], device_id=sibling,
        device_id_type=MESH,
    ).wait_send()


def fused(projections, partner):
    rows, width = projections.shape
    groups = lax.axis_size(("dp", "sub"))
    chips = groups // 2
    pair = 2 * rows
    loss, grad = pl.pallas_call(
        functools.partial(kernel, groups),
        out_shape=(
            jax.ShapeDtypeStruct((1, 1), jnp.float32),
            jax.ShapeDtypeStruct((rows, width), jnp.float32),
        ),
        in_specs=[pl.BlockSpec(memory_space=pl.ANY)] * 2,
        out_specs=(
            pl.BlockSpec(memory_space=pltpu.SMEM),
            pl.BlockSpec(memory_space=pltpu.VMEM),
        ),
        scratch_shapes=[
            pltpu.VMEM((rows, width), jnp.float32),
            pltpu.VMEM((2, 1, rows), jnp.int32),
            pltpu.VMEM((groups, rows, width), jnp.bfloat16),
            pltpu.VMEM((chips, rows, pair), jnp.float32),
            pltpu.VMEM((groups, 1, pair + LANES), jnp.float32),
            pltpu.VMEM((2 * LANES, LANES), jnp.float32),
            pltpu.VMEM((rows, width), jnp.float32),
            pltpu.VMEM((rows, width), jnp.float32),
            pltpu.VMEM((rows, LANES), jnp.int32),
            pltpu.VMEM((rows, pair), jnp.int32),
            pltpu.SemaphoreType.DMA((2,)),
            pltpu.SemaphoreType.DMA,
            pltpu.SemaphoreType.DMA((groups,)),
            pltpu.SemaphoreType.DMA,
            pltpu.SemaphoreType.DMA((chips,)),
            pltpu.SemaphoreType.DMA,
            pltpu.SemaphoreType.DMA,
            pltpu.SemaphoreType.REGULAR,
            pltpu.SemaphoreType.REGULAR,
            pltpu.SemaphoreType.REGULAR,
        ],
        compiler_params=pltpu.CompilerParams(collective_id=0, has_side_effects=True),
    )(projections, partner.reshape(1, rows))
    return loss.reshape(()), grad


def general(projections, partner):
    rows = projections.shape[0]
    axes = ("dp", "sub")
    inverse = lax.rsqrt(jnp.sum(projections * projections, axis=1) + EPS)
    unit = projections * inverse[:, None]
    low = unit.astype(jnp.bfloat16)
    everyone = lax.all_gather(low, axes, axis=0, tiled=True)
    columns = jnp.arange(everyone.shape[0], dtype=jnp.int32)
    ids = lax.axis_index(axes) * rows + jnp.arange(rows, dtype=jnp.int32)
    score = (
        lax.dot_general(
            low, everyone, (((1,), (1,)), ((), ())), preferred_element_type=jnp.float32
        )
        / TAU
    )
    diag = columns[None, :] == ids[:, None]
    hit = columns[None, :] == partner[:, None]
    total = jnp.sum(jnp.where(diag, 0.0, jnp.exp(score - SHIFT)), axis=1)
    found = jnp.sum(jnp.where(hit, score, 0.0), axis=1)
    lse = jnp.log(total) + SHIFT
    lse_all = lax.all_gather(lse, axes, axis=0, tiled=True)
    loss = lax.psum(jnp.sum(lse - found), axes) / everyone.shape[0]
    weight = jnp.exp(score - lse[:, None]) + jnp.exp(score - lse_all[None, :])
    weight = weight - 2.0 * hit.astype(jnp.float32)
    weight = jnp.where(diag, 0.0, weight / TAU).astype(jnp.bfloat16)
    grown = jnp.dot(weight, everyone, preferred_element_type=jnp.float32)
    inner = jnp.sum(unit * grown, axis=1)
    return loss, inverse[:, None] * (grown - unit * inner[:, None])


def solution(mesh):
    small = mesh.shape["dp"] == 4 * LINE and mesh.shape["sub"] == 2

    def body(projections, partner):
        rows, width = projections.shape
        fits = width == LANES and LANES < rows < 2 * LANES and (2 * rows) % LANES == 0
        return (fused if small and fits else general)(projections, partner)

    return jax.shard_map(
        body,
        mesh=mesh,
        in_specs=(P(("dp", "sub"), None), P(("dp", "sub"))),
        out_specs=(P(), P(("dp", "sub"), None)),
        check_vma=False,
    )
```

time: 30.9 us -> 27.4 us (0.89)
  Pallas kernels: 26.7 us -> 23.2 us
    pallas_call x1, Pallas kernels: 26.7 us -> 23.2 us  [fused(): pl.pallas_call(functools.partial(kernel, groups), out_shape=(jax.ShapeDty...]
where the time goes in v1:
time: 27.4 us; the launch traced here: 27.2 us
  Pallas kernels  23.2 us (85%)
  between operations  2.45 us (9%)
  local copies, waits for them, and re-layouts  1.54 us (6%)
    pallas_call x1, Pallas kernels, fused(): pl.pallas_call(functools.partial(kernel, groups), out_shape=(jax.ShapeDty...  23.2 us
    unnamed x1, local copies, waits for them, and re-layouts  1.54 us

profile of v1, /device:TPU:0, one launch (start us, length us, event | category | flops | bytes accessed | tf_op | source)
XLA Modules:
  0.0 27.2 jit_solution(12296731735251009073)
XLA Ops:
  0.6 23.2 %shard_map.41 = (f32[1,1]{1,0:T(1,128)}, f32[192,128]{1,0:T(8,128)}) custom-call(f32[192,128]{1,0:T(8,128)} %p_hbm.1, s32[1,192]{1,0:T(1,128)} %bitcast.2), custom_call_target="tpu_custom_call" | custom-call | tf_op jit(solution)/shard_map/pallas_call | solution.py:292
  24.5 1.5 %copy.7 = f32[192,128]{1,0:T(8,128)} copy(f32[192,128]{1,0:T(8,128)} %get-tuple-element.9) | data formatting | bytes 196608
